TPU v7x, 512 devices: a 8x2x16 block of a 8x8x16 slice. The times are simulated.
512 devices in a mesh: groups: 2 (over y), seg: 32 (over z, core), bin: 8 (over x).
Axes of the slice: x: 8, y: 2, z: 16, core: 2. Of those that a mesh axis runs over, the one named last changes fastest.
The devices are a block of a 8x8x16 slice.
Arguments:
- start_factors: float32 [32768, 128], P(('groups', 'seg', 'bin')), parts along dimension 0, may hold values from -6 to 6
- bin_factors: bfloat16 [16384, 128], P(('groups', 'bin')), parts along dimension 0, may hold values from -0.5 to 0.5
- tile_speed: bfloat16 [64, 8, 12, 128, 128], P(('groups', 'seg'), 'bin'), parts along dimension 0, may hold values from -6 to 6
- tile_weight: bfloat16 [64, 8, 12, 128, 128], P(('groups', 'seg'), 'bin'), parts along dimension 0, may hold values from 0.099609375 to 2
- tile_cells: int32 [64, 8, 12, 2], P(('groups', 'seg'), 'bin'), parts along dimension 0, may hold values from 0 to 7, as said below
- tile_count: int32 [64, 8], P(('groups', 'seg'), 'bin'), parts along dimension 0, may hold values from 1 to 12, as said below
- inner_pairs: int32 [64, 8, 2, 2], P(('groups', 'seg'), 'bin'), parts along dimension 0, may hold values from 0 to 3, as said below
- inner_weight: float32 [64, 8, 2, 128, 128], P(('groups', 'seg'), 'bin'), parts along dimension 0, may hold values from 0 to 0.00390625
- face_rows: int32 [64, 8, 2, 256], P(('groups', 'seg'), 'bin'), parts along dimension 0, may hold values from 0 to 511, as said below
- face_count: int32 [64, 8, 2], P(('groups', 'seg'), 'bin'), parts along dimension 0, may hold values from 128 to 256, as said below
- face_weight: float32 [64, 8, 256, 256], P(('groups', 'seg'), 'bin'), parts along dimension 0, may hold values from 0 to 0.00390625
Outputs:
- solution_factors: float32 [32768, 128], P(('groups', 'seg', 'bin')), parts along dimension 0
- residual: float32 [32768, 128], P(('groups', 'seg', 'bin')), parts along dimension 0
There are 2 independent parts, one for each index of `groups`. A program takes and returns all parts, laid end to end along the dimension named above; each array names one. Nothing has to cross between parts.
Inputs may be any that keep to these rules, and one draw needn't show every extreme that they name: `tile_cells`: the 12 slots of one device name different pairs; the first entry is a segment block of the partition, the second a bin block of the device's bins. `tile_count`: some device of every draw has all 12 slots live. `inner_pairs`: the two blocks of a pair differ; both are segment blocks of the partition. `face_rows`: row numbers within the partition, different within each face list. `face_count`: some face list of every draw has all 256 rows live.
All inputs are finite; a program needn't handle non-finite values.
Results may differ from a plain program's by a relative error of at most 0.0024.
Values sent between devices are 32-bit elements; how exact they have to be, the bound alone decides.
A program may use at most 64 MiB of HBM per device.

v0:
```python
import jax
import jax.numpy as jnp
from jax import lax
from jax.sharding import Mesh
from jax.sharding import PartitionSpec as P

ITERS = 2
SEG = ("seg_0", "seg_1")
SEG_BIN = ("seg_0", "seg_1", "bin")
GROUPS_SEG_BIN = ("groups", "seg_0", "seg_1", "bin")
GROUPS_SEG = ("groups", "seg_0", "seg_1")
highest = lax.Precision.HIGHEST
ridge_weight = 0.5


def from_behind(x, axis, by):
    devices = lax.axis_size(axis)
    pairs = [(i, i + by) for i in range(devices) if 0 <= i + by < devices]
    return lax.ppermute(x, axis, pairs)


def cut_along(x, dim, devices):
    before, after = (x.shape[:dim], x.shape[dim + 1 :])
    return jnp.moveaxis(x.reshape(*before, devices, -1, *after), dim, 0)


def sent_and_summed(x, axis, dim):
    devices = lax.axis_size(axis)
    blocks = lax.all_to_all(cut_along(x, dim, devices), axis, 0, 0, tiled=True)
    return jnp.sum(blocks, axis=0)


def in_order(blocks, dim):
    shape = list(blocks.shape[1:])
    shape[dim] *= blocks.shape[0]
    return jnp.moveaxis(blocks, 0, dim).reshape(shape)


def sent_to_all(x, axis):
    devices = lax.axis_size(axis)
    return lax.all_to_all(jnp.broadcast_to(x[None], (devices, *x.shape)), axis, 0, 0, tiled=True)


def gathered_copies(x, axis, dim):
    return in_order(sent_to_all(x, axis), dim)


def one_axis_at_a_time(x, axes):
    for axis in axes:
        x = lax.psum(x, axis)
    return x


def shards(
    start_factors,
    bin_factors,
    tile_speed,
    tile_weight,
    tile_cells,
    tile_count,
    inner_pairs,
    inner_weight,
    face_rows,
    face_count,
    face_weight,
):
    speeds = tile_speed[0, 0]
    weights = tile_weight[0, 0]
    cells = tile_cells[0, 0]
    n_tiles = speeds.shape[0]
    tile_size = speeds.shape[1]
    own_rows = start_factors.shape[0]
    width = start_factors.shape[1]
    part_rows = own_rows * lax.axis_size("bin")
    part_blocks = part_rows // tile_size
    block_ids = jnp.arange(part_blocks, dtype=jnp.int32)
    live_tiles = (jnp.arange(n_tiles, dtype=jnp.int32) < tile_count[0, 0]).astype(jnp.float32)
    tile_bins = bin_factors.reshape(-1, tile_size, width)[cells[:, 1]]
    bins_wide = tile_bins.astype(jnp.float32)
    tile_gain = weights.astype(jnp.float32) * live_tiles[:, None, None]
    tile_onehot = (cells[:, 0][:, None] == block_ids[None, :]).astype(jnp.float32)
    weighted = (weights.astype(jnp.float32) * speeds.astype(jnp.float32)).astype(jnp.bfloat16)
    rhs_terms = jnp.einsum("kij,kjr->kir", weighted, tile_bins, preferred_element_type=jnp.float32)
    rhs_terms = rhs_terms * live_tiles[:, None, None]
    rhs_part = jnp.einsum("kb,kir->bir", tile_onehot, rhs_terms, precision=highest).reshape(
        part_rows, width
    )
    pairs = inner_pairs[0, 0]
    pair_weight = inner_weight[0, 0]
    left_onehot = (pairs[:, 0][:, None] == block_ids[None, :]).astype(jnp.float32)
    right_onehot = (pairs[:, 1][:, None] == block_ids[None, :]).astype(jnp.float32)
    left_degree = pair_weight.sum(2)
    right_degree = pair_weight.sum(1)
    rows_low = face_rows[0, 0, 0]
    rows_up = face_rows[0, 0, 1]
    face_slots = jnp.arange(rows_low.shape[0], dtype=jnp.int32)
    mask_low = (face_slots < face_count[0, 0, 0]).astype(jnp.float32)
    mask_up = (face_slots < face_count[0, 0, 1]).astype(jnp.float32)
    upper_count = face_count[0, 0, 1:2]
    face_block = face_weight[0, 0]

    def apply_local(whole_rows):
        blocks = whole_rows.reshape(part_blocks, tile_size, width)
        picked = blocks[cells[:, 0]]
        scores = jnp.einsum("kir,kjr->kij", picked, bins_wide, precision=highest) * tile_gain
        pulled = jnp.einsum("kij,kjr->kir", scores, bins_wide, precision=highest)
        left = blocks[pairs[:, 0]]
        right = blocks[pairs[:, 1]]
        to_left = left_degree[..., None] * left - jnp.einsum(
            "kij,kjr->kir", pair_weight, right, precision=highest
        )
        to_right = right_degree[..., None] * right - jnp.einsum(
            "kij,kir->kjr", pair_weight, left, precision=highest
        )
        summed = jnp.einsum("kb,kir->bir", tile_onehot, pulled, precision=highest)
        summed = summed + jnp.einsum("kb,kir->bir", left_onehot, to_left, precision=highest)
        summed = summed + jnp.einsum("kb,kir->bir", right_onehot, to_right, precision=highest)
        summed = summed.reshape(part_rows, width)
        own_face = whole_rows[rows_low] * mask_low[:, None]
        upper_face = whole_rows[rows_up] * mask_up[:, None]
        lower_face, lower_count = from_behind((upper_face, upper_count), SEG, 1)
        lower_mask = (face_slots < lower_count[0]).astype(jnp.float32)
        coupling = face_block * mask_low[:, None] * lower_mask[None, :]
        own_term = coupling.sum(1)[:, None] * own_face - jnp.dot(
            coupling, lower_face, precision=highest
        )
        answer = coupling.sum(0)[:, None] * lower_face - jnp.dot(
            coupling.T, own_face, precision=highest
        )
        returned = from_behind(answer, SEG, -1)
        return summed.at[rows_low].add(own_term).at[rows_up].add(returned)

    def reduce_rows(partial_value):
        reduced = sent_and_summed(partial_value, "bin", 0)
        return reduced

    def spread(vector):
        whole_rows = gathered_copies(vector, "bin", 0)
        return whole_rows

    def fold_sum(values):
        folded = (one_axis_at_a_time(values[0], SEG_BIN), one_axis_at_a_time(values[1], SEG_BIN))
        return folded

    def image_of(vector):
        return reduce_rows(apply_local(spread(vector))) + ridge_weight * vector

    start_whole = gathered_copies(start_factors, "bin", 0)
    residual = reduce_rows(rhs_part - apply_local(start_whole)) - ridge_weight * start_factors
    solution = start_factors
    images = image_of(residual)
    norm_now, product = fold_sum((jnp.sum(residual * residual), jnp.sum(residual * images)))
    step_size = norm_now / product
    direction = residual
    along = images
    for iteration in range(ITERS):
        solution = solution + step_size * direction
        residual = residual - step_size * along
        if iteration + 1 < ITERS:
            images = image_of(residual)
            norm_next, product = fold_sum(
                (jnp.sum(residual * residual), jnp.sum(residual * images))
            )
            beta_ratio = norm_next / norm_now
            step_size = norm_next / (product - beta_ratio * norm_next / step_size)
            direction = residual + beta_ratio * direction
            along = images + beta_ratio * along
            norm_now = norm_next
    outputs = (solution, residual)
    return outputs


def solution(mesh):
    finer = Mesh(
        mesh.devices.reshape(mesh.shape["groups"], 16, 2, mesh.shape["bin"]),
        ("groups", "seg_0", "seg_1", "bin"),
    )
    in_specs = (
        P(GROUPS_SEG_BIN, None),
        P(("groups", "bin"), None),
        P(GROUPS_SEG, "bin", None, None, None),
        P(GROUPS_SEG, "bin", None, None, None),
        P(GROUPS_SEG, "bin", None, None),
        P(GROUPS_SEG, "bin"),
        P(GROUPS_SEG, "bin", None, None),
        P(GROUPS_SEG, "bin", None, None, None),
        P(GROUPS_SEG, "bin", None, None),
        P(GROUPS_SEG, "bin", None),
        P(GROUPS_SEG, "bin", None, None),
    )
    out_specs = (P(GROUPS_SEG_BIN, None), P(GROUPS_SEG_BIN, None))
    return jax.shard_map(
        shards, mesh=finer, in_specs=in_specs, out_specs=out_specs, check_vma=False
    )
```

profile of v0, /device:TPU:80, one launch (start us, length us, event | category | flops | bytes accessed | tf_op | source)
XLA Modules:
  0.0 300.7 jit_solution(3569220163104865625)
XLA Ops:
  0.6 1.5 broadcast_in_dim.6
  2.2 7.4 %all-to-all-start = ((f32[8,64,128]{2,1,0:T(8,128)}), f32[8,64,128]{2,1,0:T(8,128)S(1)}, u32[]{:S(2)}, u32[]{:S(2)}) async-start(f32[8,64,128]{2,1,0:T(8,128)} %broadcast_in_dim.6), calls=%async_computation | async-start | bytes 524288 | tf_op jit(solution)/shard_map/all_to_all | solution.py:41
  10.2 2.2 collective-permute-start
  26.3 5.6 %collective-permute-start.1 = (f32[256,128]{1,0:T(8,128)S(1)}, f32[256,128]{1,0:T(8,128)S(1)}, u32[]{:S(2)}, u32[]{:S(2)}) collective-permute-start(f32[256,128]{1,0:T(8,128)S(1)} %broadcast_multiply_fusion.2), channel_id=1, source_target_pairs={{0,8},{8,16},{16,24},{24,32},{32,40},{40,48},{48,56},{56,64},{64,7... | collective-permute-start | bytes 393224 | tf_op jit(solution)/shard_map/ppermute | solution.py:19
  39.1 2.0 scatter_fusion
  41.2 2.0 scatter_fusion.1
  43.3 17.7 %all_to_all.30 = f32[8,64,128]{2,1,0:T(8,128)S(1)} all-to-all(f32[8,64,128]{2,1,0:T(8,128)S(1)} %bitcast.164), channel_id=1, replica_groups=mesh['groups'=2,'seg_0'=16,'seg_1'=2,'bin'=8] {'bin'}, dimensions={0} | all-to-all | bytes 524288 | tf_op jit(solution)/shard_map/all_to_all | solution.py:29
  61.8 13.7 %all_to_all.31 = f32[8,64,128]{2,1,0:T(8,128)S(1)} all-to-all(f32[8,64,128]{2,1,0:T(8,128)S(1)} %broadcast_in_dim.7), channel_id=1, replica_groups=mesh['groups'=2,'seg_0'=16,'seg_1'=2,'bin'=8] {'bin'}, dimensions={0} | all-to-all | bytes 524288 | tf_op jit(solution)/shard_map/all_to_all | solution.py:41
  80.5 4.0 %collective-permute-start.3 = (f32[256,128]{1,0:T(8,128)S(1)}, f32[256,128]{1,0:T(8,128)S(1)}, u32[]{:S(2)}, u32[]{:S(2)}) collective-permute-start(f32[256,128]{1,0:T(8,128)S(1)} %broadcast_multiply_fusion.1), channel_id=1, source_target_pairs={{0,8},{8,16},{16,24},{24,32},{32,40},{40,48},{48,56},{56,64},{64,7... | collective-permute-start | bytes 393224 | tf_op jit(solution)/shard_map/ppermute | solution.py:19
  90.7 2.0 scatter_fusion.2
  92.8 2.2 collective-permute-done.4
  95.0 2.0 scatter_fusion.3
  97.0 13.9 %all_to_all.32 = f32[8,64,128]{2,1,0:T(8,128)S(1)} all-to-all(f32[8,64,128]{2,1,0:T(8,128)S(1)} %bitcast.163), channel_id=1, replica_groups=mesh['groups'=2,'seg_0'=16,'seg_1'=2,'bin'=8] {'bin'}, dimensions={0} | all-to-all | bytes 524288 | tf_op jit(solution)/shard_map/all_to_all | solution.py:29
  111.5 68.4 %all-reduce.1 = (f32[]{:T(128)}, f32[]{:T(128)}) all-reduce(f32[]{:T(128)} %get-tuple-element.9, f32[]{:T(128)} %get-tuple-element.8), channel_id=1, replica_groups=mesh['groups'=2,'seg_0'=16,'seg_1'=2,'bin'=8] {'seg_0'}, use_global_device_ids=true, to_apply=%region_8.0 | all-reduce | flops 2 | bytes 16 | tf_op jit(solution)/shard_map/psum | solution.py:50
  179.9 3.1 %all-reduce.5 = (f32[]{:T(128)}, f32[]{:T(128)}) all-reduce(f32[]{:T(128)} %get-tuple-element.16, f32[]{:T(128)} %get-tuple-element.17), channel_id=1, replica_groups=mesh['groups'=2,'seg_0'=16,'seg_1'=2,'bin'=8] {'seg_1'}, use_global_device_ids=true, to_apply=%region_9.0 | all-reduce | flops 2 | bytes 16 | tf_op jit(solution)/shard_map/psum | solution.py:50
  183.0 15.5 %all-reduce.3 = (f32[]{:T(128)}, f32[]{:T(128)}) all-reduce(f32[]{:T(128)} %get-tuple-element.24, f32[]{:T(128)} %get-tuple-element.25), channel_id=1, replica_groups=mesh['groups'=2,'seg_0'=16,'seg_1'=2,'bin'=8] {'bin'}, use_global_device_ids=true, to_apply=%region_10.0 | all-reduce | flops 2 | bytes 16 | tf_op jit(solution)/shard_map/psum | solution.py:50
  199.9 14.0 %all_to_all.33 = f32[8,64,128]{2,1,0:T(8,128)S(1)} all-to-all(f32[8,64,128]{2,1,0:T(8,128)S(1)} %broadcast_in_dim.8), channel_id=1, replica_groups=mesh['groups'=2,'seg_0'=16,'seg_1'=2,'bin'=8] {'bin'}, dimensions={0} | all-to-all | bytes 524288 | tf_op jit(solution)/shard_map/all_to_all | solution.py:41
  218.3 1.5 collective-permute-start.5
  225.7 2.0 scatter_fusion.4
  229.1 2.0 scatter_fusion.5
  231.2 13.3 %all_to_all.34 = f32[8,64,128]{2,1,0:T(8,128)S(1)} all-to-all(f32[8,64,128]{2,1,0:T(8,128)S(1)} %bitcast.160), channel_id=1, replica_groups=mesh['groups'=2,'seg_0'=16,'seg_1'=2,'bin'=8] {'bin'}, dimensions={0} | all-to-all | bytes 524288 | tf_op jit(solution)/shard_map/all_to_all | solution.py:29
  245.1 31.9 %all-reduce = (f32[]{:T(128)}, f32[]{:T(128)}) all-reduce(f32[]{:T(128)} %get-tuple-element.7, f32[]{:T(128)} %get-tuple-element.6), channel_id=1, replica_groups=mesh['groups'=2,'seg_0'=16,'seg_1'=2,'bin'=8] {'seg_0'}, use_global_device_ids=true, to_apply=%region_19.0 | all-reduce | flops 2 | bytes 16 | tf_op jit(solution)/shard_map/psum | solution.py:50
  277.0 3.1 %all-reduce.4 = (f32[]{:T(128)}, f32[]{:T(128)}) all-reduce(f32[]{:T(128)} %get-tuple-element.14, f32[]{:T(128)} %get-tuple-element.15), channel_id=1, replica_groups=mesh['groups'=2,'seg_0'=16,'seg_1'=2,'bin'=8] {'seg_1'}, use_global_device_ids=true, to_apply=%region_20.0 | all-reduce | flops 2 | bytes 16 | tf_op jit(solution)/shard_map/psum | solution.py:50
  280.2 15.4 %all-reduce.2 = (f32[]{:T(128)}, f32[]{:T(128)}) all-reduce(f32[]{:T(128)} %get-tuple-element.22, f32[]{:T(128)} %get-tuple-element.23), channel_id=1, replica_groups=mesh['groups'=2,'seg_0'=16,'seg_1'=2,'bin'=8] {'bin'}, use_global_device_ids=true, to_apply=%region_21.0 | all-reduce | flops 2 | bytes 16 | tf_op jit(solution)/shard_map/psum | solution.py:50
  (151 shorter events, 46.0 us)
Async XLA Ops:
  0.6 15.3 %copy-start = (bf16[1024,128]{1,0:T(8,128)(2,1)S(1)}, bf16[1024,128]{1,0:T(8,128)(2,1)}, u32[]{:S(2)}) copy-start(bf16[1024,128]{1,0:T(8,128)(2,1)} %param.12) | copy-start | bytes 786436
  2.2 7.5 %copy-start.30 = (s32[1,1,2]{2,1,0:T(1,128)S(1)}, s32[1,1,2]{2,1,0:T(1,128)}, u32[]{:S(2)}) copy-start(s32[1,1,2]{2,1,0:T(1,128)} %param.20) | copy-start | bytes 28
  2.2 19.4 %all-to-all-start = ((f32[8,64,128]{2,1,0:T(8,128)}), f32[8,64,128]{2,1,0:T(8,128)S(1)}, u32[]{:S(2)}, u32[]{:S(2)}) async-start(f32[8,64,128]{2,1,0:T(8,128)} %broadcast_in_dim.6), calls=%async_computation | async-start | bytes 524288 | tf_op jit(solution)/shard_map/all_to_all | solution.py:41
  10.2 2.2 copy-start.31
  10.2 9.5 %collective-permute-start = (s32[1]{0:T(128)}, s32[1]{0:T(128)}, u32[]{:S(2)}, u32[]{:S(2)}) collective-permute-start(s32[1]{0:T(128)} %bitcast.23), channel_id=1, source_target_pairs={{0,8},{8,16},{16,24},{24,32},{32,40},{40,48},{48,56},{56,64},{64,7... | collective-permute-start | bytes 20 | tf_op jit(solution)/shard_map/ppermute | solution.py:19
  12.4 4.9 %copy-start.12 = (s32[12]{0:T(128)}, s32[12]{0:T(128)S(1)}, u32[]{:S(2)}) copy-start(s32[12]{0:T(128)S(1)} %get-tuple-element.30) | copy-start | bytes 148
  13.1 9.1 %copy-start.20 = (f32[12]{0:T(128)}, f32[12]{0:T(128)S(1)}, u32[]{:S(2)}) copy-start(f32[12]{0:T(128)S(1)} %compare_convert_fusion.3) | copy-start | bytes 148
  15.3 10.2 %copy-start.15 = (s32[1024]{0:T(1024)}, s32[1024]{0:T(1024)S(1)}, u32[]{:S(2)}) copy-start(s32[1024]{0:T(1024)S(1)} %pad_clamp_fusion) | copy-start | bytes 12292
  15.9 5.6 %copy-start.25 = (s32[1024]{0:T(1024)}, s32[1024]{0:T(1024)S(1)}, u32[]{:S(2)}) copy-start(s32[1024]{0:T(1024)S(1)} %get-tuple-element.37) | copy-start | bytes 12292
  18.2 1.4 copy-start.2
  18.2 2.1 copy-start.1
  18.3 5.3 %copy-start.27 = (s32[1024]{0:T(1024)}, s32[1024]{0:T(1024)S(1)}, u32[]{:S(2)}) copy-start(s32[1024]{0:T(1024)S(1)} %get-tuple-element.36) | copy-start | bytes 12292
  18.3 5.9 %copy-start.26 = (s32[1024]{0:T(1024)}, s32[1024]{0:T(1024)S(1)}, u32[]{:S(2)}) copy-start(s32[1024]{0:T(1024)S(1)} %get-tuple-element.35) | copy-start | bytes 12292
  19.7 5.1 %copy-start.8 = (f32[2,128]{1,0:T(2,128)}, f32[2,128]{1,0:T(2,128)S(1)}, u32[]{:S(2)}) copy-start(f32[2,128]{1,0:T(2,128)S(1)} %get-tuple-element.5) | copy-start | bytes 3076
  19.7 5.3 %copy-start.10 = (f32[2,128]{1,0:T(2,128)}, f32[2,128]{1,0:T(2,128)S(1)}, u32[]{:S(2)}) copy-start(f32[2,128]{1,0:T(2,128)S(1)} %get-tuple-element.4) | copy-start | bytes 3076
  26.3 5.6 %copy-start.22 = (s32[2]{0:T(128)S(1)}, s32[2]{0:T(128)}, u32[]{:S(2)}) copy-start(s32[2]{0:T(128)} %get-tuple-element.13) | copy-start | bytes 28
  26.3 9.7 %collective-permute-start.1 = (f32[256,128]{1,0:T(8,128)S(1)}, f32[256,128]{1,0:T(8,128)S(1)}, u32[]{:S(2)}, u32[]{:S(2)}) collective-permute-start(f32[256,128]{1,0:T(8,128)S(1)} %broadcast_multiply_fusion.2), channel_id=1, source_target_pairs={{0,8},{8,16},{16,24},{24,32},{32,40},{40,48},{48,56},{56,64},{64,7... | collective-permute-start | bytes 393224 | tf_op jit(solution)/shard_map/ppermute | solution.py:19
  37.4 3.8 %collective-permute-start.2 = (f32[256,128]{1,0:T(8,128)S(1)}, f32[256,128]{1,0:T(8,128)S(1)}, u32[]{:S(2)}, u32[]{:S(2)}) collective-permute-start(f32[256,128]{1,0:T(8,128)S(1)} %multiply_subtract_fusion.2), channel_id=1, source_target_pairs={{8,0},{16,8},{24,16},{32,24},{40,32},{48,40},{56,48},{64,56},{72,6... | collective-permute-start | bytes 393224 | tf_op jit(solution)/shard_map/ppermute | solution.py:19
  61.8 13.7 %copy-start.16 = (s32[1024]{0:T(1024)S(1)}, s32[1024]{0:T(1024)}, u32[]{:S(2)}) copy-start(s32[1024]{0:T(1024)} %copy-done.15) | copy-start | bytes 12292
  80.4 4.1 %copy-start.21 = (f32[12]{0:T(128)S(1)}, f32[12]{0:T(128)}, u32[]{:S(2)}) copy-start(f32[12]{0:T(128)} %copy-done.20) | copy-start | bytes 148
  80.5 7.8 %collective-permute-start.3 = (f32[256,128]{1,0:T(8,128)S(1)}, f32[256,128]{1,0:T(8,128)S(1)}, u32[]{:S(2)}, u32[]{:S(2)}) collective-permute-start(f32[256,128]{1,0:T(8,128)S(1)} %broadcast_multiply_fusion.1), channel_id=1, source_target_pairs={{0,8},{8,16},{16,24},{24,32},{32,40},{40,48},{48,56},{56,64},{64,7... | collective-permute-start | bytes 393224 | tf_op jit(solution)/shard_map/ppermute | solution.py:19
  89.0 6.0 %collective-permute-start.4 = (f32[256,128]{1,0:T(8,128)S(1)}, f32[256,128]{1,0:T(8,128)S(1)}, u32[]{:S(2)}, u32[]{:S(2)}) collective-permute-start(f32[256,128]{1,0:T(8,128)S(1)} %multiply_subtract_fusion.1), channel_id=1, source_target_pairs={{8,0},{16,8},{24,16},{32,24},{40,32},{48,40},{56,48},{64,56},{72,6... | collective-permute-start | bytes 393224 | tf_op jit(solution)/shard_map/ppermute | solution.py:19
  218.3 5.0 %collective-permute-start.5 = (f32[256,128]{1,0:T(8,128)S(1)}, f32[256,128]{1,0:T(8,128)S(1)}, u32[]{:S(2)}, u32[]{:S(2)}) collective-permute-start(f32[256,128]{1,0:T(8,128)S(1)} %broadcast_multiply_fusion), channel_id=1, source_target_pairs={{0,8},{8,16},{16,24},{24,32},{32,40},{40,48},{48,56},{56,64},{64,7... | collective-permute-start | bytes 393224 | tf_op jit(solution)/shard_map/ppermute | solution.py:19
  224.0 5.2 %collective-permute-start.6 = (f32[256,128]{1,0:T(8,128)S(1)}, f32[256,128]{1,0:T(8,128)S(1)}, u32[]{:S(2)}, u32[]{:S(2)}) collective-permute-start(f32[256,128]{1,0:T(8,128)S(1)} %multiply_subtract_fusion), channel_id=1, source_target_pairs={{8,0},{16,8},{24,16},{32,24},{40,32},{48,40},{56,48},{64,56},{72,6... | collective-permute-start | bytes 393224 | tf_op jit(solution)/shard_map/ppermute | solution.py:19
  (16 other events, 12.3 us)
where the time goes:
time: 302 us; the launch traced here: 301 us
  blocking collectives  210 us (70%)
  starting transfers between devices  24.7 us (8%)
  other arithmetic  19.4 us (6%)
  local copies, waits for them, and re-layouts  18.1 us (6%)
  matrix products  16.6 us (5%)
  between operations  7.96 us (3%)
  waiting for transfers between devices  3.97 us (1%)
    psum x6, blocking collectives, one_axis_at_a_time(): x = lax.psum(x, axis)  137 us
    all_to_all x3, blocking collectives, sent_and_summed(): blocks = lax.all_to_all(cut_along(x, dim, devices), axis, 0, 0, tiled=True)  44.9 us
    all_to_all x2, blocking collectives, sent_to_all(): lax.all_to_all(jnp.broadcast_to(x[None], (devices, *x.shape)), axis, 0, 0...  27.7 us
    ppermute x7, starting transfers between devices, from_behind(): return lax.ppermute(x, axis, pairs)  17.2 us
    scatter-add x6, other arithmetic, apply_local(): return summed.at[rows_low].add(own_term).at[rows_up].add(returned)  12.3 us
    all_to_all x1, starting transfers between devices, sent_to_all(): lax.all_to_all(jnp.broadcast_to(x[None], (devices, *x.shape)), axis, 0, 0...  7.45 us
  transfers between devices with their start and end apart: 8, of which 3 were waited for; matrix products, arithmetic and copies ran while one was open for 8% of the time, Pallas kernels for 0%

commit v1 on v0

--- a/solution.py
+++ b/solution.py
@@ -13,6 +13,12 @@
 ridge_weight = 0.5
 
 
+def summed_here(block, axis):
+    parts = lax.all_gather(block, axis, axis=0, tiled=False)
+    total = parts.sum(axis=0)
+    return total
+
+
 def from_behind(x, axis, by):
     devices = lax.axis_size(axis)
     pairs = [(i, i + by) for i in range(devices) if 0 <= i + by < devices]
@@ -47,7 +53,7 @@
 
 def one_axis_at_a_time(x, axes):
     for axis in axes:
-        x = lax.psum(x, axis)
+        x = summed_here(x, axis)
     return x
 
 

time: 302 us -> 327 us (1.083)
  blocking collectives: 210 us -> 176 us
  local copies, waits for them, and re-layouts: 18.1 us -> 38.7 us
  waiting for transfers between devices: 3.97 us -> 20.7 us
  starting transfers between devices: 24.7 us -> 35.5 us
  other arithmetic: 19.4 us -> 30.1 us
    psum x6 -> x0, blocking collectives: 137 us -> none  [one_axis_at_a_time(): x = lax.psum(x, axis)]
    unnamed x0 -> x6, blocking collectives: none -> 135 us
    all_to_all x3 -> x1, blocking collectives: 44.9 us -> 13.3 us  [sent_and_summed(): blocks = lax.all_to_all(cut_along(x, dim, devices), axis, 0, 0, tiled=True)]
    unnamed x64 -> x91, local copies, waits for them, and re-layouts: 4.98 us -> 24.9 us
    all_to_all x0 -> x2, waiting for transfers between devices: none -> 18.7 us  [sent_and_summed(): blocks = lax.all_to_all(cut_along(x, dim, devices), axis, 0, 0, tiled=True)]
    all_to_all x0 -> x2, starting transfers between devices: none -> 10.8 us  [sent_and_summed(): blocks = lax.all_to_all(cut_along(x, dim, devices), axis, 0, 0, tiled=True)]
    reduce_sum x0 -> x12, other arithmetic: none -> 7.28 us  [summed_here(): total = parts.sum(axis=0)]
  transfers between devices with their start and end apart: 8 -> 10, of which waited for: 3 -> 5; matrix products, arithmetic and copies ran while one was open for 8% -> 9% of each run, Pallas kernels for 0% -> 0%
where the time goes in v1:
time: 327 us; the launch traced here: 326 us
  blocking collectives  176 us (54%)
  local copies, waits for them, and re-layouts  38.7 us (12%)
  starting transfers between devices  35.5 us (11%)
  other arithmetic  30.1 us (9%)
  waiting for transfers between devices  20.7 us (6%)
  matrix products  16.6 us (5%)
  between operations  7.94 us (2%)
    unnamed x6, blocking collectives  135 us
    all_to_all x2, blocking collectives, sent_to_all(): lax.all_to_all(jnp.broadcast_to(x[None], (devices, *x.shape)), axis, 0, 0...  27.6 us
    unnamed x91, local copies, waits for them, and re-layouts  24.9 us
    all_to_all x2, waiting for transfers between devices, sent_and_summed(): blocks = lax.all_to_all(cut_along(x, dim, devices), axis, 0, 0, tiled=True)  18.7 us
    ppermute x7, starting transfers between devices, from_behind(): return lax.ppermute(x, axis, pairs)  17.2 us
    scatter-add x6, other arithmetic, apply_local(): return summed.at[rows_low].add(own_term).at[rows_up].add(returned)  15 us
    all_to_all x1, blocking collectives, sent_and_summed(): blocks = lax.all_to_all(cut_along(x, dim, devices), axis, 0, 0, tiled=True)  13.3 us
    all_to_all x2, starting transfers between devices, sent_and_summed(): blocks = lax.all_to_all(cut_along(x, dim, devices), axis, 0, 0, tiled=True)  10.8 us
  transfers between devices with their start and end apart: 10, of which 5 were waited for; matrix products, arithmetic and copies ran while one was open for 9% of the time, Pallas kernels for 0%

profile of v1, /device:TPU:80, one launch (start us, length us, event | category | flops | bytes accessed | tf_op | source)
XLA Modules:
  0.0 325.8 jit_solution(2740752290227529239)
XLA Ops:
  2.2 7.4 %all-to-all-start = ((f32[8,64,128]{2,1,0:T(8,128)}), f32[8,64,128]{2,1,0:T(8,128)S(1)}, u32[]{:S(2)}, u32[]{:S(2)}) async-start(f32[8,64,128]{2,1,0:T(8,128)} %broadcast_in_dim.6), calls=%async_computation | async-start | bytes 524288 | tf_op jit(solution)/shard_map/all_to_all | solution.py:47
  10.2 2.2 collective-permute-start
  26.3 5.6 %collective-permute-start.1 = (f32[256,128]{1,0:T(8,128)S(1)}, f32[256,128]{1,0:T(8,128)S(1)}, u32[]{:S(2)}, u32[]{:S(2)}) collective-permute-start(f32[256,128]{1,0:T(8,128)S(1)} %broadcast_multiply_fusion.2), channel_id=1, source_target_pairs={{0,8},{8,16},{16,24},{24,32},{32,40},{40,48},{48,56},{56,64},{64,7... | collective-permute-start | bytes 393224 | tf_op jit(solution)/shard_map/ppermute | solution.py:25
  39.1 2.0 scatter_fusion
  41.2 2.0 scatter_fusion.1
  44.0 7.2 %all-to-all-start.1 = ((f32[8,64,128]{2,1,0:T(8,128)}), f32[8,64,128]{2,1,0:T(8,128)S(1)}, u32[]{:S(2)}, u32[]{:S(2)}) async-start(f32[8,64,128]{2,1,0:T(8,128)} %bitcast.29), calls=%async_computation.1 | async-start | bytes 524288 | tf_op jit(solution)/shard_map/all_to_all | solution.py:35
  51.2 10.7 %all-to-all-done.1 = f32[8,64,128]{2,1,0:T(8,128)S(1)} async-done(((f32[8,64,128]{2,1,0:T(8,128)}), f32[8,64,128]{2,1,0:T(8,128)S(1)}, u32[]{:S(2)}, u32[]{:S(2)}) %all-to-all-start.1) | async-done | bytes 262176 | tf_op jit(solution)/shard_map/all_to_all | solution.py:35
  62.0 13.7 %all_to_all.30 = f32[8,64,128]{2,1,0:T(8,128)S(1)} all-to-all(f32[8,64,128]{2,1,0:T(8,128)S(1)} %broadcast_in_dim.7), channel_id=1, replica_groups=mesh['groups'=2,'seg_0'=16,'seg_1'=2,'bin'=8] {'bin'}, dimensions={0} | all-to-all | bytes 524288 | tf_op jit(solution)/shard_map/all_to_all | solution.py:47
  80.7 4.0 %collective-permute-start.3 = (f32[256,128]{1,0:T(8,128)S(1)}, f32[256,128]{1,0:T(8,128)S(1)}, u32[]{:S(2)}, u32[]{:S(2)}) collective-permute-start(f32[256,128]{1,0:T(8,128)S(1)} %broadcast_multiply_fusion.1), channel_id=1, source_target_pairs={{0,8},{8,16},{16,24},{24,32},{32,40},{40,48},{48,56},{56,64},{64,7... | collective-permute-start | bytes 393224 | tf_op jit(solution)/shard_map/ppermute | solution.py:25
  91.6 3.4 %scatter_fusion.2 = f32[512,128]{1,0:T(8,128)} fusion(f32[512,128]{1,0:T(8,128)} %bitcast.39, s32[256]{0:T(256)S(1)} %bitcast.183, f32[256,128]{1,0:T(8,128)S(1)} %convolution_subtract_fusion.1), kind=kCustom, calls=%fused_computation.18 | custom fusion | flops 32768 | bytes 394240 | tf_op jit(solution)/shard_map/scatter-add | solution.py:137
  95.8 3.4 %scatter_fusion.3 = f32[512,128]{1,0:T(8,128)} fusion(f32[512,128]{1,0:T(8,128)} %scatter_fusion.2, s32[256]{0:T(256)S(1)} %bitcast.179, f32[256,128]{1,0:T(8,128)S(1)} %collective-permute-done.4), kind=kCustom, calls=%fused_computation.19 | custom fusion | flops 32768 | bytes 394240 | tf_op jit(solution)/shard_map/scatter-add | solution.py:137
  99.2 3.6 %all-to-all-start.3 = ((f32[8,64,128]{2,1,0:T(8,128)}), f32[8,64,128]{2,1,0:T(8,128)S(1)}, u32[]{:S(2)}, u32[]{:S(2)}) async-start(f32[8,64,128]{2,1,0:T(8,128)} %bitcast.41), calls=%async_computation.3 | async-start | bytes 524288 | tf_op jit(solution)/shard_map/all_to_all | solution.py:35
  105.4 8.0 %all-to-all-done.3 = f32[8,64,128]{2,1,0:T(8,128)S(1)} async-done(((f32[8,64,128]{2,1,0:T(8,128)}), f32[8,64,128]{2,1,0:T(8,128)S(1)}, u32[]{:S(2)}, u32[]{:S(2)}) %all-to-all-start.3) | async-done | bytes 262176 | tf_op jit(solution)/shard_map/all_to_all | solution.py:35
  117.1 69.0 %all-reduce.13 = (f32[16]{0:T(128)S(1)}, f32[16]{0:T(128)S(1)}) all-reduce(f32[16]{0:T(128)S(1)} %dynamic-update-slice, f32[16]{0:T(128)S(1)} %dynamic-update-slice.3), channel_id=1, replica_groups=mesh['groups'=2,'seg_0'=16,'seg_1'=2,'bin'=8] {'seg_0'}, use_global_device_ids=true, to_apply=%add | all-reduce | flops 32 | bytes 256
  191.3 2.5 all-reduce.17
  197.8 14.8 %all-reduce.15 = (f32[8]{0:T(128)S(1)}, f32[8]{0:T(128)S(1)}) all-reduce(f32[8]{0:T(128)S(1)} %dynamic-update-slice.2, f32[8]{0:T(128)S(1)} %dynamic-update-slice.5), channel_id=1, replica_groups=mesh['groups'=2,'seg_0'=16,'seg_1'=2,'bin'=8] {'bin'}, use_global_device_ids=true, to_apply=%add.2 | all-reduce | flops 16 | bytes 128
  215.0 13.9 %all_to_all.31 = f32[8,64,128]{2,1,0:T(8,128)S(1)} all-to-all(f32[8,64,128]{2,1,0:T(8,128)S(1)} %broadcast_in_dim.8), channel_id=1, replica_groups=mesh['groups'=2,'seg_0'=16,'seg_1'=2,'bin'=8] {'bin'}, dimensions={0} | all-to-all | bytes 524288 | tf_op jit(solution)/shard_map/all_to_all | solution.py:47
  233.3 1.5 collective-permute-start.5
  240.7 2.0 scatter_fusion.4
  243.5 2.0 scatter_fusion.5
  245.6 13.3 %all_to_all.32 = f32[8,64,128]{2,1,0:T(8,128)S(1)} all-to-all(f32[8,64,128]{2,1,0:T(8,128)S(1)} %bitcast.175), channel_id=1, replica_groups=mesh['groups'=2,'seg_0'=16,'seg_1'=2,'bin'=8] {'bin'}, dimensions={0} | all-to-all | bytes 524288 | tf_op jit(solution)/shard_map/all_to_all | solution.py:35
  262.4 31.8 %all-reduce.12 = (f32[16]{0:T(128)S(1)}, f32[16]{0:T(128)S(1)}) all-reduce(f32[16]{0:T(128)S(1)} %dynamic-update-slice.6, f32[16]{0:T(128)S(1)} %dynamic-update-slice.9), channel_id=1, replica_groups=mesh['groups'=2,'seg_0'=16,'seg_1'=2,'bin'=8] {'seg_0'}, use_global_device_ids=true, to_apply=%add.6 | all-reduce | flops 32 | bytes 256
  298.1 2.5 all-reduce.16
  304.6 14.8 %all-reduce.14 = (f32[8]{0:T(128)S(1)}, f32[8]{0:T(128)S(1)}) all-reduce(f32[8]{0:T(128)S(1)} %dynamic-update-slice.8, f32[8]{0:T(128)S(1)} %dynamic-update-slice.11), channel_id=1, replica_groups=mesh['groups'=2,'seg_0'=16,'seg_1'=2,'bin'=8] {'bin'}, use_global_device_ids=true, to_apply=%add.8 | all-reduce | flops 16 | bytes 128
  (192 shorter events, 76.4 us)
Async XLA Ops:
  0.6 15.3 %copy-start = (bf16[1024,128]{1,0:T(8,128)(2,1)S(1)}, bf16[1024,128]{1,0:T(8,128)(2,1)}, u32[]{:S(2)}) copy-start(bf16[1024,128]{1,0:T(8,128)(2,1)} %param.12) | copy-start | bytes 786436
  2.2 7.5 %copy-start.30 = (s32[1,1,2]{2,1,0:T(1,128)S(1)}, s32[1,1,2]{2,1,0:T(1,128)}, u32[]{:S(2)}) copy-start(s32[1,1,2]{2,1,0:T(1,128)} %param.20) | copy-start | bytes 28
  2.2 19.4 %all-to-all-start = ((f32[8,64,128]{2,1,0:T(8,128)}), f32[8,64,128]{2,1,0:T(8,128)S(1)}, u32[]{:S(2)}, u32[]{:S(2)}) async-start(f32[8,64,128]{2,1,0:T(8,128)} %broadcast_in_dim.6), calls=%async_computation | async-start | bytes 524288 | tf_op jit(solution)/shard_map/all_to_all | solution.py:47
  10.2 9.5 %collective-permute-start = (s32[1]{0:T(128)}, s32[1]{0:T(128)}, u32[]{:S(2)}, u32[]{:S(2)}) collective-permute-start(s32[1]{0:T(128)} %bitcast.23), channel_id=1, source_target_pairs={{0,8},{8,16},{16,24},{24,32},{32,40},{40,48},{48,56},{56,64},{64,7... | collective-permute-start | bytes 20 | tf_op jit(solution)/shard_map/ppermute | solution.py:25
  12.4 4.9 %copy-start.12 = (s32[12]{0:T(128)}, s32[12]{0:T(128)S(1)}, u32[]{:S(2)}) copy-start(s32[12]{0:T(128)S(1)} %get-tuple-element.30) | copy-start | bytes 148
  13.1 9.1 %copy-start.20 = (f32[12]{0:T(128)}, f32[12]{0:T(128)S(1)}, u32[]{:S(2)}) copy-start(f32[12]{0:T(128)S(1)} %compare_convert_fusion.3) | copy-start | bytes 148
  15.3 10.2 %copy-start.15 = (s32[1024]{0:T(1024)}, s32[1024]{0:T(1024)S(1)}, u32[]{:S(2)}) copy-start(s32[1024]{0:T(1024)S(1)} %pad_clamp_fusion) | copy-start | bytes 12292
  15.9 5.6 %copy-start.25 = (s32[1024]{0:T(1024)}, s32[1024]{0:T(1024)S(1)}, u32[]{:S(2)}) copy-start(s32[1024]{0:T(1024)S(1)} %get-tuple-element.37) | copy-start | bytes 12292
  18.3 5.3 %copy-start.27 = (s32[1024]{0:T(1024)}, s32[1024]{0:T(1024)S(1)}, u32[]{:S(2)}) copy-start(s32[1024]{0:T(1024)S(1)} %get-tuple-element.36) | copy-start | bytes 12292
  18.3 5.9 %copy-start.26 = (s32[1024]{0:T(1024)}, s32[1024]{0:T(1024)S(1)}, u32[]{:S(2)}) copy-start(s32[1024]{0:T(1024)S(1)} %get-tuple-element.35) | copy-start | bytes 12292
  19.7 5.1 %copy-start.8 = (f32[2,128]{1,0:T(2,128)}, f32[2,128]{1,0:T(2,128)S(1)}, u32[]{:S(2)}) copy-start(f32[2,128]{1,0:T(2,128)S(1)} %get-tuple-element.5) | copy-start | bytes 3076
  19.7 5.3 %copy-start.10 = (f32[2,128]{1,0:T(2,128)}, f32[2,128]{1,0:T(2,128)S(1)}, u32[]{:S(2)}) copy-start(f32[2,128]{1,0:T(2,128)S(1)} %get-tuple-element.4) | copy-start | bytes 3076
  26.3 5.6 %copy-start.22 = (s32[2]{0:T(128)S(1)}, s32[2]{0:T(128)}, u32[]{:S(2)}) copy-start(s32[2]{0:T(128)} %get-tuple-element.13) | copy-start | bytes 28
  26.3 9.7 %collective-permute-start.1 = (f32[256,128]{1,0:T(8,128)S(1)}, f32[256,128]{1,0:T(8,128)S(1)}, u32[]{:S(2)}, u32[]{:S(2)}) collective-permute-start(f32[256,128]{1,0:T(8,128)S(1)} %broadcast_multiply_fusion.2), channel_id=1, source_target_pairs={{0,8},{8,16},{16,24},{24,32},{32,40},{40,48},{48,56},{56,64},{64,7... | collective-permute-start | bytes 393224 | tf_op jit(solution)/shard_map/ppermute | solution.py:25
  37.4 3.8 %collective-permute-start.2 = (f32[256,128]{1,0:T(8,128)S(1)}, f32[256,128]{1,0:T(8,128)S(1)}, u32[]{:S(2)}, u32[]{:S(2)}) collective-permute-start(f32[256,128]{1,0:T(8,128)S(1)} %multiply_subtract_fusion.2), channel_id=1, source_target_pairs={{8,0},{16,8},{24,16},{32,24},{40,32},{48,40},{56,48},{64,56},{72,6... | collective-permute-start | bytes 393224 | tf_op jit(solution)/shard_map/ppermute | solution.py:25
  44.0 17.9 %all-to-all-start.1 = ((f32[8,64,128]{2,1,0:T(8,128)}), f32[8,64,128]{2,1,0:T(8,128)S(1)}, u32[]{:S(2)}, u32[]{:S(2)}) async-start(f32[8,64,128]{2,1,0:T(8,128)} %bitcast.29), calls=%async_computation.1 | async-start | bytes 524288 | tf_op jit(solution)/shard_map/all_to_all | solution.py:35
  51.2 10.7 %copy-start.5 = (f32[64,128]{1,0:T(8,128)S(1)}, f32[64,128]{1,0:T(8,128)}, u32[]{:S(2)}) copy-start(f32[64,128]{1,0:T(8,128)} %param.11) | copy-start | bytes 98308
  62.0 13.7 %copy-start.16 = (s32[1024]{0:T(1024)S(1)}, s32[1024]{0:T(1024)}, u32[]{:S(2)}) copy-start(s32[1024]{0:T(1024)} %copy-done.15) | copy-start | bytes 12292
  80.6 4.1 %copy-start.21 = (f32[12]{0:T(128)S(1)}, f32[12]{0:T(128)}, u32[]{:S(2)}) copy-start(f32[12]{0:T(128)} %copy-done.20) | copy-start | bytes 148
  80.7 8.4 %collective-permute-start.3 = (f32[256,128]{1,0:T(8,128)S(1)}, f32[256,128]{1,0:T(8,128)S(1)}, u32[]{:S(2)}, u32[]{:S(2)}) collective-permute-start(f32[256,128]{1,0:T(8,128)S(1)} %broadcast_multiply_fusion.1), channel_id=1, source_target_pairs={{0,8},{8,16},{16,24},{24,32},{32,40},{40,48},{48,56},{56,64},{64,7... | collective-permute-start | bytes 393224 | tf_op jit(solution)/shard_map/ppermute | solution.py:25
  89.8 6.0 %collective-permute-start.4 = (f32[256,128]{1,0:T(8,128)S(1)}, f32[256,128]{1,0:T(8,128)S(1)}, u32[]{:S(2)}, u32[]{:S(2)}) collective-permute-start(f32[256,128]{1,0:T(8,128)S(1)} %multiply_subtract_fusion.1), channel_id=1, source_target_pairs={{8,0},{16,8},{24,16},{32,24},{40,32},{48,40},{56,48},{64,56},{72,6... | collective-permute-start | bytes 393224 | tf_op jit(solution)/shard_map/ppermute | solution.py:25
  99.2 14.2 %all-to-all-start.3 = ((f32[8,64,128]{2,1,0:T(8,128)}), f32[8,64,128]{2,1,0:T(8,128)S(1)}, u32[]{:S(2)}, u32[]{:S(2)}) async-start(f32[8,64,128]{2,1,0:T(8,128)} %bitcast.41), calls=%async_computation.3 | async-start | bytes 524288 | tf_op jit(solution)/shard_map/all_to_all | solution.py:35
  233.3 5.0 %collective-permute-start.5 = (f32[256,128]{1,0:T(8,128)S(1)}, f32[256,128]{1,0:T(8,128)S(1)}, u32[]{:S(2)}, u32[]{:S(2)}) collective-permute-start(f32[256,128]{1,0:T(8,128)S(1)} %broadcast_multiply_fusion), channel_id=1, source_target_pairs={{0,8},{8,16},{16,24},{24,32},{32,40},{40,48},{48,56},{56,64},{64,7... | collective-permute-start | bytes 393224 | tf_op jit(solution)/shard_map/ppermute | solution.py:25
  239.0 4.6 %collective-permute-start.6 = (f32[256,128]{1,0:T(8,128)S(1)}, f32[256,128]{1,0:T(8,128)S(1)}, u32[]{:S(2)}, u32[]{:S(2)}) collective-permute-start(f32[256,128]{1,0:T(8,128)S(1)} %multiply_subtract_fusion), channel_id=1, source_target_pairs={{8,0},{16,8},{24,16},{32,24},{40,32},{48,40},{56,48},{64,56},{72,6... | collective-permute-start | bytes 393224 | tf_op jit(solution)/shard_map/ppermute | solution.py:25
  (18 other events, 17.3 us)
